TPU v7x, 16 devices: a 4x2x1 block of a 4x4x8 slice. The times are simulated.
16 devices in a mesh: dp: 4 (over y, z, core), tp: 4 (over x).
Axes of the slice: x: 4, y: 2, z: 1, core: 2. Of those that a mesh axis runs over, the one named last changes fastest.
The devices are a block of a 4x4x8 slice.
Arguments:
- x: bfloat16 [8192, 2048], P('dp'), parts along dimension 0
- w_gate: bfloat16 [2048, 8192], P(None, 'tp')
- w_up: bfloat16 [2048, 8192], P(None, 'tp')
- w_down: bfloat16 [8192, 2048], P('tp')
Outputs:
- output: bfloat16 [8192, 2048], P('dp'), parts along dimension 0
There are 4 independent parts. A program takes and returns all parts, laid end to end along the dimension named above; an argument that names none is the same for every part.
All inputs are finite; a program needn't handle non-finite values.
Results may differ from a plain program's by a relative error of at most 0.016.
Values are sent between devices in bfloat16 or wider.
A program may use at most 768 MiB of HBM per device.

v0:
```python
import jax
import jax.numpy as jnp
from jax import lax
from jax.sharding import PartitionSpec as P


def solution(mesh):
    def step(x, w_gate, w_up, w_down):
        gate = jnp.dot(x, w_gate, preferred_element_type=jnp.float32)
        up = jnp.dot(x, w_up, preferred_element_type=jnp.float32)
        hidden = (jax.nn.silu(gate) * up).astype(jnp.bfloat16)
        term = jnp.dot(hidden, w_down, preferred_element_type=jnp.float32).astype(jnp.bfloat16)
        return lax.psum(term, "tp")

    return jax.shard_map(
        step,
        mesh=mesh,
        in_specs=(P("dp", None), P(None, "tp"), P(None, "tp"), P("tp", None)),
        out_specs=P("dp", None),
        check_vma=False,
    )
```

profile of v0, /device:TPU:112, one launch (start us, length us, event | category | flops | bytes accessed | tf_op | source)
XLA Modules:
  0.0 247.4 jit_solution(11634916028771578661)
XLA Ops:
  6.5 0.0 all-reduce.2.cloned.1.call-start
  6.6 0.0 copy-start
  6.6 0.0 copy-start.1
  6.6 24.3 %fusion.1 = f32[2048,2048]{1,0:T(8,128)} fusion(bf16[2048,2048]{1,0:T(8,128)(2,1)} %param.4, bf16[2048,2048]{1,0:T(8,128)(2,1)} %param.5), kind=kOutput, calls=%fused_computation.3 | convolution fusion | flops 17179869184 | bytes 33554432 | tf_op jit(solution)/shard_map/dot_general | solution.py:9
  30.8 0.0 copy-done
  30.8 0.0 copy-done.1
  30.8 22.9 %multiply_convert_fusion.clone.4 = bf16[2048,2048]{1,0:T(8,128)(2,1)} fusion(f32[2048,2048]{1,0:T(8,128)} %fusion.1, bf16[2048,2048]{1,0:T(8,128)(2,1)S(1)} %copy-done, bf16[2048,2048]{1,0:T(8,128)(2,1)S(1)} %copy-done.1), kind=kOutput, calls=%fused_computation.clone.clone.clone.1 | convolution fusion | flops 17205035008 | bytes 41943040 | tf_op jit(solution)/shard_map/dot_general | solution.py:10
  53.7 23.6 %convolution_convert_fusion = bf16[2048,2048]{1,0:T(8,128)(2,1)} fusion(bf16[2048,2048]{1,0:T(8,128)(2,1)} %param.7, bf16[2048,2048]{1,0:T(8,128)(2,1)} %multiply_convert_fusion.clone.4), kind=kOutput, calls=%fused_computation.1 | convolution fusion | flops 17184063488 | bytes 25165824 | tf_op jit(solution)/shard_map/dot_general | solution.py:12
  77.3 0.1 all-reduce.2.cloned.1.call-update
  77.4 154.8 %all-reduce.2.cloned.1.call-done = bf16[2048,2048]{1,0:T(8,128)(2,1)} async-done(((bf16[2048,2048]{1,0:T(8,128)(2,1)}), bf16[2048,2048]{1,0:T(8,128)(2,1)}) %all-reduce.2.cloned.1.call-update) | async-done | bytes 8388624 | tf_op jit(solution)/shard_map/psum | solution.py:13
  232.1 8.4 %copy.6 = bf16[2048,2048]{1,0:T(8,128)(2,1)} copy(bf16[2048,2048]{1,0:T(8,128)(2,1)} %all-reduce.2.cloned.1.call-done) | data formatting | bytes 16777216
Async XLA Ops:
  6.5 225.6 %all-reduce.2.cloned.1.call-start = ((), (), s32[]{:S(2)}) async-start(), calls=%async_computation | async-start | bytes 16777216 | tf_op jit(solution)/shard_map/psum | solution.py:13
  6.6 24.3 %copy-start = (bf16[2048,2048]{1,0:T(8,128)(2,1)S(1)}, bf16[2048,2048]{1,0:T(8,128)(2,1)}, u32[]{:S(2)}) copy-start(bf16[2048,2048]{1,0:T(8,128)(2,1)} %param.4) | copy-start | bytes 25165828
  6.6 24.3 %copy-start.1 = (bf16[2048,2048]{1,0:T(8,128)(2,1)S(1)}, bf16[2048,2048]{1,0:T(8,128)(2,1)}, u32[]{:S(2)}) copy-start(bf16[2048,2048]{1,0:T(8,128)(2,1)} %param.6) | copy-start | bytes 25165828
Sparse Core Ops, SparseCore 0:
  77.5 154.6 all-reduce.1
where the time goes:
time: 248 us; the launch traced here: 247 us
  waiting for transfers between devices  155 us (62%)
  matrix products  70.7 us (29%)
  between operations  13.4 us (5%)
  local copies, waits for them, and re-layouts  8.45 us (3%)
    psum x1, waiting for transfers between devices, step(): return lax.psum(term, 'tp')  155 us
    dot_general x1, matrix products, step(): gate = jnp.dot(x, w_gate, preferred_element_type=jnp.float32)  24.3 us
    dot_general x1, matrix products, step(): jnp.dot(hidden, w_down, preferred_element_type=jnp.float32)  23.6 us
    dot_general x1, matrix products, step(): up = jnp.dot(x, w_up, preferred_element_type=jnp.float32)  22.9 us
    unnamed x5, local copies, waits for them, and re-layouts  8.45 us
  transfers between devices with their start and end apart: 1, of which 1 were waited for; matrix products, arithmetic and copies ran while one was open for 0% of the time, Pallas kernels for 0%

commit v1 on v0

v1 whole, which is shorter than its diff:
```python
import functools

import jax
import jax.numpy as jnp
from jax import lax
from jax.experimental import pallas as pl
from jax.experimental.pallas import tpu as pltpu
from jax.sharding import PartitionSpec as P

COLS = 512


def kernel(x_ref, wg_ref, wu_ref, wd_ref, y_ref, xbuf, wg, wu, wd, hid, sbuf, rbuf, own, fin,
           x_sem, w_sem, d_sem, send_sem, recv_sem, ag_send, ag_recv, loc_sem):
    n = 4
    me = lax.axis_index("tp")
    right, left = lax.rem(me + 1, n), lax.rem(me + n - 1, n)
    rows, depth = x_ref.shape
    width = wg_ref.shape[1]
    chunk = rows // n
    half = chunk // 2
    sub = half // 2
    steps = width // COLS
    dsteps = wd_ref.shape[1] // COLS

    def row_of(owner, part, s):
        return pl.multiple_of(lax.rem(owner, n) * chunk + part * half + s * sub, sub)

    def x_copies(p):
        kind, s, slot = p // 2, lax.rem(p, 2), lax.rem(p, 2)
        r = row_of(me + (4 - kind) // 2, lax.rem(kind + 1, 2), s)
        l = row_of(me + 2 + (kind + 1) // 2, lax.rem(kind, 2), s)
        return (
            pltpu.make_async_copy(x_ref.at[pl.ds(r, sub)], xbuf.at[slot, pl.ds(0, sub)], x_sem.at[slot, 0]),
            pltpu.make_async_copy(x_ref.at[pl.ds(l, sub)], xbuf.at[slot, pl.ds(sub, sub)], x_sem.at[slot, 1]),
        )

    def w_copies(c):
        cols = pl.ds(pl.multiple_of(c * COLS, COLS), COLS)
        return (
            pltpu.make_async_copy(wg_ref.at[:, cols], wg.at[:, cols], w_sem.at[c, 0]),
            pltpu.make_async_copy(wu_ref.at[:, cols], wu.at[:, cols], w_sem.at[c, 1]),
        )

    def d_copy(c):
        cols = pl.ds(pl.multiple_of(c * COLS, COLS), COLS)
        return pltpu.make_async_copy(wd_ref.at[:, cols], wd.at[:, cols], d_sem.at[c])

    def remote(src, dst, ssem, rsem, to):
        return pltpu.make_async_remote_copy(
            src_ref=src, dst_ref=dst, send_sem=ssem, recv_sem=rsem,
            device_id={"tp": to}, device_id_type=pl.DeviceIdType.MESH)

    def rs_copies(kind, s):
        p = 2 * kind + s
        lo, hi = pl.ds(0, sub), pl.ds(sub, sub)
        dr, dl = (hi, lo) if kind == 2 else (lo, hi)
        return (
            remote(sbuf.at[p, lo], rbuf.at[kind, s, dr], send_sem.at[p, 0], recv_sem.at[p, 0], right),
            remote(sbuf.at[p, hi], rbuf.at[kind, s, dl], send_sem.at[p, 1], recv_sem.at[p, 1], left),
        )

    for c in x_copies(0):
        c.start()
    for c in range(steps):
        for w in w_copies(c):
            w.start()
    for c in range(dsteps):
        d_copy(c).start()

    barrier = pltpu.get_barrier_semaphore()
    for to in (left, right):
        pl.semaphore_signal(barrier, inc=1, device_id={"tp": to}, device_id_type=pl.DeviceIdType.MESH)
    pl.semaphore_wait(barrier, 2)

    def run_pass(kind, s, first):
        p = 2 * kind + s
        slot = s
        for c in x_copies(p):
            c.wait()

        @pl.when(p < 7)
        def _():
            for c in x_copies(p + 1):
                c.start()

        def up_step(c, _):
            @pl.when(first)
            def _():
                for w in w_copies(c):
                    w.wait()
            cols = pl.ds(pl.multiple_of(c * COLS, COLS), COLS)
            xv = xbuf[slot]
            g = jnp.dot(xv, wg[:, cols], preferred_element_type=jnp.float32)
            u = jnp.dot(xv, wu[:, cols], preferred_element_type=jnp.float32)
            hid[:, cols] = (jax.nn.silu(g) * u).astype(jnp.bfloat16)
            return 0

        lax.fori_loop(0, steps, up_step, 0)

        if kind >= 2:
            for c in rs_copies(kind - 2, s):
                c.wait_recv()

        def down_step(c, _):
            @pl.when(first)
            def _():
                d_copy(c).wait()
            cols = pl.ds(pl.multiple_of(c * COLS, COLS), COLS)
            t = jnp.dot(hid[...], wd[:, cols], preferred_element_type=jnp.float32)
            if kind >= 2:
                t = t + rbuf[kind - 2, s, :, cols].astype(jnp.float32)
            if kind < 3:
                sbuf[p, :, cols] = t.astype(jnp.bfloat16)
            else:
                own[s, :, cols] = t
            return 0

        lax.fori_loop(0, dsteps, down_step, 0)
        if kind < 3:
            for c in rs_copies(kind, s):
                c.start()

    for kind in range(4):
        def body(s, _, kind=kind):
            run_pass(kind, s, (s == 0) if kind == 0 else False)
            return 0
        lax.fori_loop(0, 2, body, 0)

    def ag(src, owner, part, s, d, slot):
        at = pl.ds(row_of(owner, part, s), sub)
        return remote(src, y_ref.at[at], ag_send.at[s, d, slot], ag_recv.at[s, d, slot], (right, left)[d])

    def finished(part, s):
        return fin.at[s, pl.ds(part * sub, sub)]

    def local(part, s):
        return pltpu.make_async_copy(finished(part, s), y_ref.at[pl.ds(row_of(me, part, s), sub)], loc_sem.at[s, part])

    for s in range(2):
        for c in rs_copies(2, s):
            c.wait_recv()
        fin[s] = (own[s] + rbuf[2, s].astype(jnp.float32)).astype(jnp.bfloat16)
        for part in range(2):
            for d in range(2):
                q = part if d == 0 else 1 - part
                ag(finished(q, s), me, q, s, d, q).start()
        for part in range(2):
            local(part, s).start()

    def forward(s, d):
        owner = left if d == 0 else right
        at = pl.ds(row_of(owner, d, s), sub)
        return ag(y_ref.at[at], owner, d, s, d, 2)

    for s in range(2):
        for d in range(2):
            ag(finished(d, s), me, d, s, d, d).wait_recv()
            forward(s, d).start()
    for s in range(2):
        for d in range(2):
            ag(finished(1 - d, s), me, 1 - d, s, d, 1 - d).wait_recv()
            forward(s, d).wait_recv()
    for s in range(2):
        for part in range(2):
            local(part, s).wait()
        for kind in range(3):
            for c in rs_copies(kind, s):
                c.wait_send()
        for d in range(2):
            for q in range(2):
                ag(finished(q, s), me, q, s, d, q).wait_send()
            forward(s, d).wait_send()


def solution(mesh):
    n = mesh.shape["tp"]
    assert n == 4

    def step(x, w_gate, w_up, w_down):
        rows, depth = x.shape
        width, out = w_down.shape
        block = rows // n // 2
        bf16, f32 = jnp.bfloat16, jnp.float32
        any_ = pl.BlockSpec(memory_space=pl.ANY)
        dma = pltpu.SemaphoreType.DMA
        return pl.pallas_call(
            kernel,
            out_shape=jax.ShapeDtypeStruct((rows, out), bf16),
            in_specs=[any_] * 4,
            out_specs=any_,
            scratch_shapes=[
                pltpu.VMEM((2, block, depth), bf16),
                pltpu.VMEM((depth, width), bf16),
                pltpu.VMEM((depth, width), bf16),
                pltpu.VMEM((width, out), bf16),
                pltpu.VMEM((block, width), bf16),
                pltpu.VMEM((6, block, out), bf16),
                pltpu.VMEM((3, 2, block, out), bf16),
                pltpu.VMEM((2, block, out), f32),
                pltpu.VMEM((2, block, out), bf16),
                dma((2, 2)),
                dma((width // COLS, 2)),
                dma((out // COLS,)),
                dma((6, 2)),
                dma((6, 2)),
                dma((2, 2, 3)),
                dma((2, 2, 3)),
                dma((2, 2)),
            ],
            compiler_params=pltpu.CompilerParams(
                collective_id=0, has_side_effects=True, vmem_limit_bytes=56 * 2**20
            ),
            cost_estimate=pl.CostEstimate(
                flops=6 * rows * depth * width, bytes_accessed=2 * (2 * rows * depth + 3 * depth * width), transcendentals=rows * width),
            name="mlp_block",
        )(x, w_gate, w_up, w_down)

    return jax.shard_map(
        step,
        mesh=mesh,
        in_specs=(P("dp", None), P(None, "tp"), P(None, "tp"), P("tp", None)),
        out_specs=P("dp", None),
        check_vma=False,
    )
```

time: 248 us -> 164 us (0.66)
  Pallas kernels: 0 us -> 155 us
  waiting for transfers between devices: 155 us -> 0 us
  matrix products: 70.7 us -> 0 us
  between operations: 13.4 us -> 0.01 us
    pallas_call x0 -> x1, Pallas kernels: none -> 155 us  [step(): pl.pallas_call(kernel, out_shape=jax.ShapeDtypeStruct((rows, out), bf16),...]
    psum x1 -> x0, waiting for transfers between devices: 155 us -> none  [step(): return lax.psum(term, 'tp')]
    dot_general x3 -> x0, matrix products: 70.7 us -> none  [the longest x1 24.3 us: step(): gate = jnp.dot(x, w_gate, preferred_element_type=jnp.float32)]
    unnamed x5 -> x1, local copies, waits for them, and re-layouts: 8.45 us -> 8.44 us
  transfers between devices with their start and end apart: 1 -> 0, of which waited for: 1 -> 0; matrix products, arithmetic and copies ran while one was open for 0% -> 0% of each run, Pallas kernels for 0% -> 0%
where the time goes in v1:
time: 164 us
  Pallas kernels  155 us (95%)
  local copies, waits for them, and re-layouts  8.44 us (5%)
    pallas_call x1, Pallas kernels, step(): pl.pallas_call(kernel, out_shape=jax.ShapeDtypeStruct((rows, out), bf16),...  155 us
    unnamed x1, local copies, waits for them, and re-layouts  8.44 us

profile of v1, /device:TPU:112, one launch (start us, length us, event | category | flops | bytes accessed | tf_op | source)
XLA Modules:
  0.0 163.9 jit_solution(9061140185609400440)
XLA Ops:
  0.0 155.4 %mlp_block.1 = bf16[2048,2048]{1,0:T(8,128)(2,1)} custom-call(bf16[2048,2048]{1,0:T(8,128)(2,1)} %x_ref.1, bf16[2048,2048]{1,0:T(8,128)(2,1)} %wg_ref.1, bf16[2048,2048]{1,0:T(8,128)(2,1)} %wu_ref.1, bf16[2048,2048]{1,0:T(8,128)(2,1)} %wd_ref.1), custom_call_target="tpu_custom_call" | custom-call | flops 51539607552 | bytes 41943040 | tf_op jit(solution)/shard_map/mlp_block/pallas_call | solution.py:187
  155.5 8.4 %copy.6 = bf16[2048,2048]{1,0:T(8,128)(2,1)} copy(bf16[2048,2048]{1,0:T(8,128)(2,1)} %mlp_block.1) | data formatting | bytes 16777216

commit v2 on v1

--- a/solution.py
+++ b/solution.py
@@ -8,10 +8,12 @@
 from jax.sharding import PartitionSpec as P
 
 COLS = 512
+LOAD = 256
+AHEAD = 3
 
 
 def kernel(x_ref, wg_ref, wu_ref, wd_ref, y_ref, xbuf, wg, wu, wd, hid, sbuf, rbuf, own, fin,
-           x_sem, w_sem, d_sem, send_sem, recv_sem, ag_send, ag_recv, loc_sem):
+           x_sem, w_sem, d_sem, send_sem, recv_sem, ag_send, ag_recv, loc_sem, first_send, first_recv):
     n = 4
     me = lax.axis_index("tp")
     right, left = lax.rem(me + 1, n), lax.rem(me + n - 1, n)
@@ -20,8 +22,8 @@
     chunk = rows // n
     half = chunk // 2
     sub = half // 2
-    steps = width // COLS
-    dsteps = wd_ref.shape[1] // COLS
+    steps, dsteps = width // COLS, wd_ref.shape[1] // COLS
+    loads, dloads = width // LOAD, wd_ref.shape[1] // LOAD
 
     def row_of(owner, part, s):
         return pl.multiple_of(lax.rem(owner, n) * chunk + part * half + s * sub, sub)
@@ -35,15 +37,18 @@
             pltpu.make_async_copy(x_ref.at[pl.ds(l, sub)], xbuf.at[slot, pl.ds(sub, sub)], x_sem.at[slot, 1]),
         )
 
+    def load_cols(c):
+        return pl.ds(pl.multiple_of(c * LOAD, LOAD), LOAD)
+
     def w_copies(c):
-        cols = pl.ds(pl.multiple_of(c * COLS, COLS), COLS)
+        cols = load_cols(c)
         return (
             pltpu.make_async_copy(wg_ref.at[:, cols], wg.at[:, cols], w_sem.at[c, 0]),
             pltpu.make_async_copy(wu_ref.at[:, cols], wu.at[:, cols], w_sem.at[c, 1]),
         )
 
     def d_copy(c):
-        cols = pl.ds(pl.multiple_of(c * COLS, COLS), COLS)
+        cols = load_cols(c)
         return pltpu.make_async_copy(wd_ref.at[:, cols], wd.at[:, cols], d_sem.at[c])
 
     def remote(src, dst, ssem, rsem, to):
@@ -51,31 +56,96 @@
             src_ref=src, dst_ref=dst, send_sem=ssem, recv_sem=rsem,
             device_id={"tp": to}, device_id_type=pl.DeviceIdType.MESH)
 
+    lo, hi = pl.ds(0, sub), pl.ds(sub, sub)
+
     def rs_copies(kind, s):
         p = 2 * kind + s
-        lo, hi = pl.ds(0, sub), pl.ds(sub, sub)
         dr, dl = (hi, lo) if kind == 2 else (lo, hi)
         return (
             remote(sbuf.at[p, lo], rbuf.at[kind, s, dr], send_sem.at[p, 0], recv_sem.at[p, 0], right),
             remote(sbuf.at[p, hi], rbuf.at[kind, s, dl], send_sem.at[p, 1], recv_sem.at[p, 1], left),
         )
 
+    def first_copies(c):
+        cols = load_cols(c)
+        return (
+            remote(sbuf.at[0, lo, cols], rbuf.at[0, 0, lo, cols], first_send.at[c, 0], first_recv.at[c, 0], right),
+            remote(sbuf.at[0, hi, cols], rbuf.at[0, 0, hi, cols], first_send.at[c, 1], first_recv.at[c, 1], left),
+        )
+
+    def gate_up(slot, cols):
+        xv = xbuf[slot]
+        g = jnp.dot(xv, wg[:, cols], preferred_element_type=jnp.float32)
+        u = jnp.dot(xv, wu[:, cols], preferred_element_type=jnp.float32)
+        hid[:, cols] = (jax.nn.silu(g) * u).astype(jnp.bfloat16)
+
     for c in x_copies(0):
         c.start()
-    for c in range(steps):
+    for c in range(AHEAD):
         for w in w_copies(c):
             w.start()
-    for c in range(dsteps):
-        d_copy(c).start()
-
+
+    def first_up(c, _):
+        for w in w_copies(c):
+            w.wait()
+
+        @pl.when(c < loads - AHEAD)
+        def _():
+            for w in w_copies(c + AHEAD):
+                w.start()
+
+        @pl.when(c >= loads - AHEAD)
+        def _():
+            d_copy(c - (loads - AHEAD)).start()
+
+        gate_up(0, load_cols(c))
+        return 0
+
+    def first_down(c, _):
+        d_copy(c).wait()
+
+        @pl.when(c < dloads - AHEAD)
+        def _():
+            d_copy(c + AHEAD).start()
+
+        cols = load_cols(c)
+        t = jnp.dot(hid[...], wd[:, cols], preferred_element_type=jnp.float32)
+        sbuf[0, :, cols] = t.astype(jnp.bfloat16)
+        for r in first_copies(c):
+            r.start()
+        return 0
+
+    for c in x_copies(0):
+        c.wait()
+    lax.fori_loop(0, loads, first_up, 0)
+    for c in x_copies(1):
+        c.start()
     barrier = pltpu.get_barrier_semaphore()
     for to in (left, right):
         pl.semaphore_signal(barrier, inc=1, device_id={"tp": to}, device_id_type=pl.DeviceIdType.MESH)
     pl.semaphore_wait(barrier, 2)
-
-    def run_pass(kind, s, first):
+    lax.fori_loop(0, dloads, first_down, 0)
+
+    def recv_wait(kind, s):
+        if kind == 0:
+            @pl.when(s == 0)
+            def _():
+                def one(c, _):
+                    for r in first_copies(c):
+                        r.wait_recv()
+                    return 0
+                lax.fori_loop(0, dloads, one, 0)
+
+            @pl.when(s > 0)
+            def _():
+                for c in rs_copies(0, s):
+                    c.wait_recv()
+        else:
+            for c in rs_copies(kind, s):
+                c.wait_recv()
+
+    def run_pass(kind, s):
         p = 2 * kind + s
-        slot = s
         for c in x_copies(p):
             c.wait()
 
@@ -84,29 +154,20 @@
             for c in x_copies(p + 1):
                 c.start()
 
+        def cols_of(c):
+            return pl.ds(pl.multiple_of(c * COLS, COLS), COLS)
+
         def up_step(c, _):
-            @pl.when(first)
-            def _():
-                for w in w_copies(c):
-                    w.wait()
-            cols = pl.ds(pl.multiple_of(c * COLS, COLS), COLS)
-            xv = xbuf[slot]
-            g = jnp.dot(xv, wg[:, cols], preferred_element_type=jnp.float32)
-            u = jnp.dot(xv, wu[:, cols], preferred_element_type=jnp.float32)
-            hid[:, cols] = (jax.nn.silu(g) * u).astype(jnp.bfloat16)
+            gate_up(s, cols_of(c))
             return 0
 
         lax.fori_loop(0, steps, up_step, 0)
 
         if kind >= 2:
-            for c in rs_copies(kind - 2, s):
-                c.wait_recv()
+            recv_wait(kind - 2, s)
 
         def down_step(c, _):
-            @pl.when(first)
-            def _():
-                d_copy(c).wait()
-            cols = pl.ds(pl.multiple_of(c * COLS, COLS), COLS)
+            cols = cols_of(c)
             t = jnp.dot(hid[...], wd[:, cols], preferred_element_type=jnp.float32)
             if kind >= 2:
                 t = t + rbuf[kind - 2, s, :, cols].astype(jnp.float32)
@@ -123,9 +184,9 @@
 
     for kind in range(4):
         def body(s, _, kind=kind):
-            run_pass(kind, s, (s == 0) if kind == 0 else False)
+            run_pass(kind, s)
             return 0
-        lax.fori_loop(0, 2, body, 0)
+        lax.fori_loop(1 if kind == 0 else 0, 2, body, 0)
 
     def ag(src, owner, part, s, d, slot):
         at = pl.ds(row_of(owner, part, s), sub)
@@ -161,12 +222,19 @@
         for d in range(2):
             ag(finished(1 - d, s), me, 1 - d, s, d, 1 - d).wait_recv()
             forward(s, d).wait_recv()
+    def first_sent(c, _):
+        for r in first_copies(c):
+            r.wait_send()
+        return 0
+
+    lax.fori_loop(0, dloads, first_sent, 0)
     for s in range(2):
         for part in range(2):
             local(part, s).wait()
         for kind in range(3):
-            for c in rs_copies(kind, s):
-                c.wait_send()
+            if kind + s > 0:
+                for c in rs_copies(kind, s):
+                    c.wait_send()
         for d in range(2):
             for q in range(2):
                 ag(finished(q, s), me, q, s, d, q).wait_send()
@@ -186,7 +254,7 @@
         dma = pltpu.SemaphoreType.DMA
         return pl.pallas_call(
             kernel,
-            out_shape=jax.ShapeDtypeStruct((rows, out), bf16),
+            out_shape=pltpu.VMEM((rows, out), bf16),
             in_specs=[any_] * 4,
             out_specs=any_,
             scratch_shapes=[
@@ -200,16 +268,18 @@
                 pltpu.VMEM((2, block, out), f32),
                 pltpu.VMEM((2, block, out), bf16),
                 dma((2, 2)),
-                dma((width // COLS, 2)),
-                dma((out // COLS,)),
+                dma((width // LOAD, 2)),
+                dma((out // LOAD,)),
                 dma((6, 2)),
                 dma((6, 2)),
                 dma((2, 2, 3)),
                 dma((2, 2, 3)),
                 dma((2, 2)),
+                dma((out // LOAD, 2)),
+                dma((out // LOAD, 2)),
             ],
             compiler_params=pltpu.CompilerParams(
-                collective_id=0, has_side_effects=True, vmem_limit_bytes=56 * 2**20
+                collective_id=0, has_side_effects=True, vmem_limit_bytes=52 * 2**20
             ),
             cost_estimate=pl.CostEstimate(
                 flops=6 * rows * depth * width, bytes_accessed=2 * (2 * rows * depth + 3 * depth * width), transcendentals=rows * width),

time: 164 us -> 154 us (0.939)
  local copies, waits for them, and re-layouts: 8.44 us -> 3.4 us
  Pallas kernels: 155 us -> 151 us
    unnamed x1, local copies, waits for them, and re-layouts: 8.44 us -> 3.4 us
    pallas_call x1, Pallas kernels: 155 us -> 151 us  [step(): pl.pallas_call(kernel, out_shape=pltpu.VMEM((rows, out), bf16), in_specs=...]
where the time goes in v2:
time: 154 us
  Pallas kernels  151 us (98%)
  local copies, waits for them, and re-layouts  3.4 us (2%)
    pallas_call x1, Pallas kernels, step(): pl.pallas_call(kernel, out_shape=pltpu.VMEM((rows, out), bf16), in_specs=...  151 us
    unnamed x1, local copies, waits for them, and re-layouts  3.4 us

profile of v2, /device:TPU:112, one launch (start us, length us, event | category | flops | bytes accessed | tf_op | source)
XLA Modules:
  0.0 154.3 jit_solution(13914577922031943477)
XLA Ops:
  0.0 150.9 %mlp_block.1 = bf16[2048,2048]{1,0:T(8,128)(2,1)S(1)} custom-call(bf16[2048,2048]{1,0:T(8,128)(2,1)} %x_ref.1, bf16[2048,2048]{1,0:T(8,128)(2,1)} %wg_ref.1, bf16[2048,2048]{1,0:T(8,128)(2,1)} %wu_ref.1, bf16[2048,2048]{1,0:T(8,128)(2,1)} %wd_ref.1), custom_call_target="tpu_custom_call" | custom-call | flops 51539607552 | bytes 41943040 | tf_op jit(solution)/shard_map/mlp_block/pallas_call | solution.py:255
  150.9 3.4 %copy.6 = bf16[2048,2048]{1,0:T(8,128)(2,1)} copy(bf16[2048,2048]{1,0:T(8,128)(2,1)S(1)} %mlp_block.1) | data formatting | bytes 16777216

commit v3 on v0

v3 whole, which is shorter than its diff:
```python
import jax
import jax.numpy as jnp
from jax import lax
from jax.experimental import pallas as pl
from jax.experimental.pallas import tpu as pltpu
from jax.sharding import PartitionSpec as P

COLS = 512
UP = (512, 512, 512, 512)
DOWN = (512, 512, 512, 512)
AHEAD = 3
MINI = 4
MINI_SEND = 1024


def kernel(x_ref, wg_ref, wu_ref, wd_ref, y_ref, xmini, xbuf, wg, wu, wd, hid, sbuf, rbuf, own,
           xm_sem, x_sem, w_sem, d_sem, ms_sem, mr_sem, send_sem, recv_sem, ag_send, ag_recv):
    n = 4
    me = lax.axis_index("tp")
    right, left = lax.rem(me + 1, n), lax.rem(me + n - 1, n)
    rows = x_ref.shape[0]
    width, out = wd_ref.shape
    chunk = rows // n
    half = chunk // 2
    sub = half // 2
    mini = half // MINI

    def row_of(owner, part, at, size):
        return pl.ds(pl.multiple_of(lax.rem(owner, n) * chunk + part * half + at, size), size)

    def remote(src, dst, ssem, rsem, to):
        return pltpu.make_async_remote_copy(
            src_ref=src, dst_ref=dst, send_sem=ssem, recv_sem=rsem,
            device_id={"tp": to}, device_id_type=pl.DeviceIdType.MESH)

    def x_pair(kind, at, size, buf, sem):
        r = row_of(me + (4 - kind) // 2, lax.rem(kind + 1, 2), at, size)
        l = row_of(me + 2 + (kind + 1) // 2, lax.rem(kind, 2), at, size)
        return (
            pltpu.make_async_copy(x_ref.at[r], buf.at[pl.ds(0, size)], sem.at[0]),
            pltpu.make_async_copy(x_ref.at[l], buf.at[pl.ds(size, size)], sem.at[1]),
        )

    def x_mini(q):
        slot = lax.rem(q, 2)
        return x_pair(0, q * mini, mini, xmini.at[slot], xm_sem.at[slot])

    def x_pass(p):
        slot = lax.rem(p, 2)
        return x_pair(p // 2, slot * sub, sub, xbuf.at[slot], x_sem.at[slot])

    def w_copies(c):
        cols = pl.ds(sum(UP[:c]), UP[c])
        return (
            pltpu.make_async_copy(wg_ref.at[:, cols], wg.at[:, cols], w_sem.at[c, 0]),
            pltpu.make_async_copy(wu_ref.at[:, cols], wu.at[:, cols], w_sem.at[c, 1]),
        )

    def d_copy(c):
        cols = pl.ds(sum(DOWN[:c]), DOWN[c])
        return pltpu.make_async_copy(wd_ref.at[:, cols], wd.at[:, cols], d_sem.at[c])

    def mini_rows(q, d):
        return pl.ds(pl.multiple_of(lax.rem(q, 2) * mini + d * sub, mini), mini)

    def mini_copies(q, cols=slice(None)):
        s = q // 2
        return tuple(
            remote(sbuf.at[s, mini_rows(q, d), cols], rbuf.at[0, s, mini_rows(q, d), cols],
                   ms_sem.at[q, d], mr_sem.at[q, d], (right, left)[d])
            for d in range(2))

    def pass_copies(kind, s, cols=slice(None)):
        p = 2 * kind + s
        return tuple(
            remote(sbuf.at[p, pl.ds(d * sub, sub), cols],
                   rbuf.at[kind, s, pl.ds((1 - d if kind == 2 else d) * sub, sub), cols],
                   send_sem.at[p, d], recv_sem.at[p, d], (right, left)[d])
            for d in range(2))

    def gate_up(xv, cols):
        m = xv.shape[0]
        g = jnp.dot(xv, wg[:, cols], preferred_element_type=jnp.float32)
        u = jnp.dot(xv, wu[:, cols], preferred_element_type=jnp.float32)
        hid[pl.ds(0, m), cols] = (jax.nn.silu(g) * u).astype(jnp.bfloat16)

    def down(m, cols):
        return jnp.dot(hid[pl.ds(0, m)], wd[:, cols], preferred_element_type=jnp.float32)

    def step_cols(c):
        return pl.ds(pl.multiple_of(c * COLS, COLS), COLS)

    barrier = pltpu.get_barrier_semaphore()
    for to in (left, right):
        pl.semaphore_signal(barrier, inc=1, device_id={"tp": to}, device_id_type=pl.DeviceIdType.MESH)

    for c in x_mini(0):
        c.start()
    weights = [w_copies(c) for c in range(len(UP))] + [(d_copy(c),) for c in range(len(DOWN))]

    def load(i):
        if i < len(weights):
            for w in weights[i]:
                w.start()

    for i in range(AHEAD):
        load(i)
    for c in x_mini(1):
        c.start()

    def store_mini(q, cols):
        t = down(2 * mini, cols).astype(jnp.bfloat16)
        for d in range(2):
            sbuf[q // 2, mini_rows(q, d), cols] = t[d * mini:(d + 1) * mini]

    for c in x_mini(0):
        c.wait()
    for c in range(len(UP)):
        for w in w_copies(c):
            w.wait()
        load(c + AHEAD)
        gate_up(xmini[0], pl.ds(sum(UP[:c]), UP[c]))
    pl.semaphore_wait(barrier, 2)
    for c in range(len(DOWN)):
        d_copy(c).wait()
        load(len(UP) + c + AHEAD)
        cols = pl.ds(sum(DOWN[:c]), DOWN[c])
        store_mini(0, cols)
        for r in mini_copies(0, cols):
            r.start()

    def mini_pass(q, _):
        for c in x_mini(q):
            c.wait()

        @pl.when(q < MINI - 1)
        def _():
            for c in x_mini(q + 1):
                c.start()

        @pl.when(q == MINI - 1)
        def _():
            for c in x_pass(2):
                c.start()

        slot = lax.rem(q, 2)

        def up_step(c, _):
            gate_up(xmini[slot], step_cols(c))
            return 0

        lax.fori_loop(0, width // COLS, up_step, 0)

        def down_steps(b, _):
            def down_step(c, _):
                store_mini(q, step_cols(c))
                return 0

            each = MINI_SEND // COLS
            lax.fori_loop(b * each, (b + 1) * each, down_step, 0)
            for r in mini_copies(q, pl.ds(pl.multiple_of(b * MINI_SEND, MINI_SEND), MINI_SEND)):
                r.start()
            return 0

        lax.fori_loop(0, out // MINI_SEND, down_steps, 0)
        return 0

    lax.fori_loop(1, MINI, mini_pass, 0)

    def run_pass(kind, s):
        p = 2 * kind + s
        for c in x_pass(p):
            c.wait()

        @pl.when(p < 7)
        def _():
            for c in x_pass(p + 1):
                c.start()

        def up_step(c, _):
            gate_up(xbuf[s], step_cols(c))
            return 0

        lax.fori_loop(0, width // COLS, up_step, 0)

        if kind == 2:
            for j in range(MINI // 2):
                for c in mini_copies(s * (MINI // 2) + j):
                    c.wait_recv()
        if kind == 3:
            for c in pass_copies(1, s):
                c.wait_recv()

        def down_step(c, _):
            cols = step_cols(c)
            t = down(2 * sub, cols)
            if kind >= 2:
                t = t + rbuf[kind - 2, s, :, cols].astype(jnp.float32)
            if kind == 3:
                own[s, :, cols] = t
            else:
                sbuf[p, :, cols] = t.astype(jnp.bfloat16)
                for r in pass_copies(kind, s, cols):
                    r.start()
            return 0

        lax.fori_loop(0, out // COLS, down_step, 0)

    for kind in range(1, 4):
        def body(s, _, kind=kind):
            run_pass(kind, s)
            return 0
        lax.fori_loop(0, 2, body, 0)

    def ag(owner, part, s, d, slot):
        at = row_of(owner, part, s * sub, sub)
        return remote(y_ref.at[at], y_ref.at[at], ag_send.at[s, d, slot], ag_recv.at[s, d, slot], (right, left)[d])

    for s in range(2):
        for c in pass_copies(2, s):
            c.wait_recv()
        for part in range(2):
            at = pl.ds(part * sub, sub)
            y_ref[row_of(me, part, s * sub, sub), :] = (
                own[s, at] + rbuf[2, s, at].astype(jnp.float32)).astype(jnp.bfloat16)
        for i in range(2):
            for d in range(2):
                q = i if d == 0 else 1 - i
                ag(me, q, s, d, q).start()

    def forward(s, d):
        return ag(left if d == 0 else right, d, s, d, 2)

    for s in range(2):
        for d in range(2):
            ag(me, d, s, d, d).wait_recv()
            forward(s, d).start()
    for s in range(2):
        for d in range(2):
            ag(me, 1 - d, s, d, 1 - d).wait_recv()
            forward(s, d).wait_recv()
    for q in range(MINI):
        for c in mini_copies(q):
            c.wait_send()
    for s in range(2):
        for kind in range(1, 3):
            for c in pass_copies(kind, s):
                c.wait_send()
        for d in range(2):
            for q in range(2):
                ag(me, q, s, d, q).wait_send()
            forward(s, d).wait_send()


def solution(mesh):
    n = mesh.shape["tp"]
    assert n == 4

    def step(x, w_gate, w_up, w_down):
        rows, depth = x.shape
        width, out = w_down.shape
        half = rows // n // 2
        bf16, f32 = jnp.bfloat16, jnp.float32
        any_ = pl.BlockSpec(memory_space=pl.ANY)
        dma = pltpu.SemaphoreType.DMA
        return pl.pallas_call(
            kernel,
            out_shape=pltpu.VMEM((rows, out), bf16),
            in_specs=[any_] * 4,
            out_specs=pl.BlockSpec(memory_space=pltpu.VMEM),
            scratch_shapes=[
                pltpu.VMEM((2, 2 * half // MINI, depth), bf16),
                pltpu.VMEM((2, half, depth), bf16),
                pltpu.VMEM((depth, width), bf16),
                pltpu.VMEM((depth, width), bf16),
                pltpu.VMEM((width, out), bf16),
                pltpu.VMEM((half, width), bf16),
                pltpu.VMEM((6, half, out), bf16),
                pltpu.VMEM((3, 2, half, out), bf16),
                pltpu.VMEM((2, half, out), f32),
                dma((2, 2)),
                dma((2, 2)),
                dma((len(UP), 2)),
                dma((len(DOWN),)),
                dma((MINI, 2)),
                dma((MINI, 2)),
                dma((6, 2)),
                dma((6, 2)),
                dma((2, 2, 3)),
                dma((2, 2, 3)),
            ],
            compiler_params=pltpu.CompilerParams(
                collective_id=0, has_side_effects=True, vmem_limit_bytes=52 * 2**20
            ),
            cost_estimate=pl.CostEstimate(
                flops=6 * rows * depth * width, bytes_accessed=2 * (2 * rows * depth + 3 * depth * width),
                transcendentals=rows * width),
            name="mlp_block",
        )(x, w_gate, w_up, w_down)

    return jax.shard_map(
        step,
        mesh=mesh,
        in_specs=(P("dp", None), P(None, "tp"), P(None, "tp"), P("tp", None)),
        out_specs=P("dp", None),
        check_vma=False,
    )
```

time: 248 us -> 152 us (0.61)
  waiting for transfers between devices: 155 us -> 0 us
  Pallas kernels: 0 us -> 148 us
  matrix products: 70.7 us -> 0 us
  between operations: 13.4 us -> 0.01 us
  local copies, waits for them, and re-layouts: 8.45 us -> 3.4 us
    psum x1 -> x0, waiting for transfers between devices: 155 us -> none  [step(): return lax.psum(term, 'tp')]
    pallas_call x0 -> x1, Pallas kernels: none -> 148 us  [step(): pl.pallas_call(kernel, out_shape=pltpu.VMEM((rows, out), bf16), in_specs=...]
    dot_general x3 -> x0, matrix products: 70.7 us -> none  [the longest x1 24.3 us: step(): gate = jnp.dot(x, w_gate, preferred_element_type=jnp.float32)]
    unnamed x5 -> x1, local copies, waits for them, and re-layouts: 8.45 us -> 3.4 us
  transfers between devices with their start and end apart: 1 -> 0, of which waited for: 1 -> 0; matrix products, arithmetic and copies ran while one was open for 0% -> 0% of each run, Pallas kernels for 0% -> 0%
where the time goes in v3:
time: 152 us; the launch traced here: 151 us
  Pallas kernels  148 us (97%)
  local copies, waits for them, and re-layouts  3.4 us (2%)
    pallas_call x1, Pallas kernels, step(): pl.pallas_call(kernel, out_shape=pltpu.VMEM((rows, out), bf16), in_specs=...  148 us
    unnamed x1, local copies, waits for them, and re-layouts  3.4 us

profile of v3, /device:TPU:112, one launch (start us, length us, event | category | flops | bytes accessed | tf_op | source)
XLA Modules:
  0.0 151.5 jit_solution(16094155715889455808)
XLA Ops:
  0.0 148.1 %mlp_block.1 = bf16[2048,2048]{1,0:T(8,128)(2,1)S(1)} custom-call(bf16[2048,2048]{1,0:T(8,128)(2,1)} %x_ref.1, bf16[2048,2048]{1,0:T(8,128)(2,1)} %wg_ref.1, bf16[2048,2048]{1,0:T(8,128)(2,1)} %wu_ref.1, bf16[2048,2048]{1,0:T(8,128)(2,1)} %wd_ref.1), custom_call_target="tpu_custom_call" | custom-call | flops 51539607552 | bytes 41943040 | tf_op jit(solution)/shard_map/mlp_block/pallas_call | solution.py:266
  148.1 3.4 %copy.6 = bf16[2048,2048]{1,0:T(8,128)(2,1)} copy(bf16[2048,2048]{1,0:T(8,128)(2,1)S(1)} %mlp_block.1) | data formatting | bytes 16777216

commit v4 on v3

--- a/solution.py
+++ b/solution.py
@@ -6,11 +6,12 @@
 from jax.sharding import PartitionSpec as P
 
 COLS = 512
-UP = (512, 512, 512, 512)
+UP = (1024, 512, 512)
 DOWN = (512, 512, 512, 512)
-AHEAD = 3
+
 MINI = 4
 MINI_SEND = 1024
+PASS_SEND = 512
 
 
 def kernel(x_ref, wg_ref, wu_ref, wd_ref, y_ref, xmini, xbuf, wg, wu, wd, hid, sbuf, rbuf, own,
@@ -98,15 +99,11 @@
         c.start()
     weights = [w_copies(c) for c in range(len(UP))] + [(d_copy(c),) for c in range(len(DOWN))]
 
-    def load(i):
-        if i < len(weights):
-            for w in weights[i]:
-                w.start()
-
-    for i in range(AHEAD):
-        load(i)
+    for i, group in enumerate(weights):
+        for w in group:
+            w.start(priority=0 if i < len(UP) else 1)
     for c in x_mini(1):
-        c.start()
+        c.start(priority=1)
 
     def store_mini(q, cols):
         t = down(2 * mini, cols).astype(jnp.bfloat16)
@@ -118,12 +115,10 @@
     for c in range(len(UP)):
         for w in w_copies(c):
             w.wait()
-        load(c + AHEAD)
         gate_up(xmini[0], pl.ds(sum(UP[:c]), UP[c]))
     pl.semaphore_wait(barrier, 2)
     for c in range(len(DOWN)):
         d_copy(c).wait()
-        load(len(UP) + c + AHEAD)
         cols = pl.ds(sum(DOWN[:c]), DOWN[c])
         store_mini(0, cols)
         for r in mini_copies(0, cols):
@@ -200,11 +195,19 @@
                 own[s, :, cols] = t
             else:
                 sbuf[p, :, cols] = t.astype(jnp.bfloat16)
-                for r in pass_copies(kind, s, cols):
+            return 0
+
+        send = (0, PASS_SEND, out, out)[kind]
+
+        def down_steps(b, _):
+            each = send // COLS
+            lax.fori_loop(b * each, (b + 1) * each, down_step, 0)
+            if kind < 3:
+                for r in pass_copies(kind, s, pl.ds(pl.multiple_of(b * send, send), send)):
                     r.start()
             return 0
 
-        lax.fori_loop(0, out // COLS, down_step, 0)
+        lax.fori_loop(0, out // send, down_steps, 0)
 
     for kind in range(1, 4):
         def body(s, _, kind=kind):

time: 152 us -> 151 us (level)
  no operation moved by 1% of the time
where the time goes in v4:
time: 151 us
  Pallas kernels  148 us (98%)
  local copies, waits for them, and re-layouts  3.4 us (2%)
    pallas_call x1, Pallas kernels, step(): pl.pallas_call(kernel, out_shape=pltpu.VMEM((rows, out), bf16), in_specs=...  148 us
    unnamed x1, local copies, waits for them, and re-layouts  3.4 us

profile of v4, /device:TPU:112, one launch (start us, length us, event | category | flops | bytes accessed | tf_op | source)
XLA Modules:
  0.0 151.0 jit_solution(17570079925888274651)
XLA Ops:
  0.0 147.6 %mlp_block.1 = bf16[2048,2048]{1,0:T(8,128)(2,1)S(1)} custom-call(bf16[2048,2048]{1,0:T(8,128)(2,1)} %x_ref.1, bf16[2048,2048]{1,0:T(8,128)(2,1)} %wg_ref.1, bf16[2048,2048]{1,0:T(8,128)(2,1)} %wu_ref.1, bf16[2048,2048]{1,0:T(8,128)(2,1)} %wd_ref.1), custom_call_target="tpu_custom_call" | custom-call | flops 51539607552 | bytes 41943040 | tf_op jit(solution)/shard_map/mlp_block/pallas_call | solution.py:269
  147.6 3.4 %copy.6 = bf16[2048,2048]{1,0:T(8,128)(2,1)} copy(bf16[2048,2048]{1,0:T(8,128)(2,1)S(1)} %mlp_block.1) | data formatting | bytes 16777216

commit v5 on v4

--- a/solution.py
+++ b/solution.py
@@ -6,12 +6,13 @@
 from jax.sharding import PartitionSpec as P
 
 COLS = 512
+WIDE = 1024
 UP = (1024, 512, 512)
 DOWN = (512, 512, 512, 512)
 
 MINI = 4
 MINI_SEND = 1024
-PASS_SEND = 512
+PASS_SEND = 1024
 
 
 def kernel(x_ref, wg_ref, wu_ref, wd_ref, y_ref, xmini, xbuf, wg, wu, wd, hid, sbuf, rbuf, own,
@@ -60,6 +61,11 @@
     def d_copy(c):
         cols = pl.ds(sum(DOWN[:c]), DOWN[c])
         return pltpu.make_async_copy(wd_ref.at[:, cols], wd.at[:, cols], d_sem.at[c])
+
+    wide = width // WIDE
+
+    def wide_cols(c):
+        return pl.ds(pl.multiple_of(c * WIDE, WIDE), WIDE)
 
     def mini_rows(q, d):
         return pl.ds(pl.multiple_of(lax.rem(q, 2) * mini + d * sub, mini), mini)
@@ -141,23 +147,19 @@
         slot = lax.rem(q, 2)
 
         def up_step(c, _):
-            gate_up(xmini[slot], step_cols(c))
-            return 0
-
-        lax.fori_loop(0, width // COLS, up_step, 0)
-
-        def down_steps(b, _):
-            def down_step(c, _):
-                store_mini(q, step_cols(c))
-                return 0
-
-            each = MINI_SEND // COLS
-            lax.fori_loop(b * each, (b + 1) * each, down_step, 0)
-            for r in mini_copies(q, pl.ds(pl.multiple_of(b * MINI_SEND, MINI_SEND), MINI_SEND)):
+            gate_up(xmini[slot], wide_cols(c))
+            return 0
+
+        lax.fori_loop(0, wide, up_step, 0)
+
+        def down_step(b, _):
+            cols = pl.ds(pl.multiple_of(b * MINI_SEND, MINI_SEND), MINI_SEND)
+            store_mini(q, cols)
+            for r in mini_copies(q, cols):
                 r.start()
             return 0
 
-        lax.fori_loop(0, out // MINI_SEND, down_steps, 0)
+        lax.fori_loop(0, out // MINI_SEND, down_step, 0)
         return 0
 
     lax.fori_loop(1, MINI, mini_pass, 0)
@@ -173,10 +175,10 @@
                 c.start()
 
         def up_step(c, _):
-            gate_up(xbuf[s], step_cols(c))
-            return 0
-
-        lax.fori_loop(0, width // COLS, up_step, 0)
+            gate_up(xbuf[s], wide_cols(c))
+            return 0
+
+        lax.fori_loop(0, wide, up_step, 0)
 
         if kind == 2:
             for j in range(MINI // 2):
@@ -186,8 +188,10 @@
             for c in pass_copies(1, s):
                 c.wait_recv()
 
+        cut = PASS_SEND if kind == 1 else WIDE
+
         def down_step(c, _):
-            cols = step_cols(c)
+            cols = pl.ds(pl.multiple_of(c * cut, cut), cut)
             t = down(2 * sub, cols)
             if kind >= 2:
                 t = t + rbuf[kind - 2, s, :, cols].astype(jnp.float32)
@@ -200,7 +204,7 @@
         send = (0, PASS_SEND, out, out)[kind]
 
         def down_steps(b, _):
-            each = send // COLS
+            each = send // cut
             lax.fori_loop(b * each, (b + 1) * each, down_step, 0)
             if kind < 3:
                 for r in pass_copies(kind, s, pl.ds(pl.multiple_of(b * send, send), send)):

time: 151 us -> 151 us (level)
  no operation moved by 1% of the time
where the time goes in v5:
time: 151 us
  Pallas kernels  148 us (98%)
  local copies, waits for them, and re-layouts  3.4 us (2%)
    pallas_call x1, Pallas kernels, step(): pl.pallas_call(kernel, out_shape=pltpu.VMEM((rows, out), bf16), in_specs=...  148 us
    unnamed x1, local copies, waits for them, and re-layouts  3.4 us

profile of v5, /device:TPU:112, one launch (start us, length us, event | category | flops | bytes accessed | tf_op | source)
XLA Modules:
  0.0 150.9 jit_solution(11011100365033782897)
XLA Ops:
  0.0 147.5 %mlp_block.1 = bf16[2048,2048]{1,0:T(8,128)(2,1)S(1)} custom-call(bf16[2048,2048]{1,0:T(8,128)(2,1)} %x_ref.1, bf16[2048,2048]{1,0:T(8,128)(2,1)} %wg_ref.1, bf16[2048,2048]{1,0:T(8,128)(2,1)} %wu_ref.1, bf16[2048,2048]{1,0:T(8,128)(2,1)} %wd_ref.1), custom_call_target="tpu_custom_call" | custom-call | flops 51539607552 | bytes 41943040 | tf_op jit(solution)/shard_map/mlp_block/pallas_call | solution.py:273
  147.5 3.4 %copy.6 = bf16[2048,2048]{1,0:T(8,128)(2,1)} copy(bf16[2048,2048]{1,0:T(8,128)(2,1)S(1)} %mlp_block.1) | data formatting | bytes 16777216
